TPU v7x, 32 devices: a whole 2x2x4 slice. The times are simulated.
32 devices in a mesh: dp: 8 (over y, x, core), tensor: 4 (over z).
Axes of the slice: x: 2, y: 2, z: 4, core: 2. Of those that a mesh axis runs over, the one named last changes fastest.
Arguments:
- hidden_in: bfloat16 [8192, 2048], P(('dp', 'tensor')), may hold values from -6 to 6
- ln_gain: bfloat16 [2048], P('dp'), may hold values from 0.25 to 1.75
- ln_bias: bfloat16 [2048], P('dp'), may hold values from -4 to 4
- qkv_weight: bfloat16 [2048, 3, 2048], P('dp', None, 'tensor'), may hold values from -0.125 to 0.125
- qkv_bias: bfloat16 [3, 32, 64], P(None, 'tensor', 'dp'), may hold values from -4 to 4
- dense_weight: bfloat16 [2048, 2048], P('tensor', 'dp'), may hold values from -0.5 to 0.5
- dense_bias: bfloat16 [2048], P('dp'), may hold values from -6 to 6
- fc1_weight: bfloat16 [2048, 8192], P('dp', 'tensor'), may hold values from -0.125 to 0.125
- fc1_bias: bfloat16 [128, 64], P('tensor', 'dp'), may hold values from -6 to 6
- fc2_weight: bfloat16 [8192, 2048], P('tensor', 'dp'), may hold values from -0.09375 to 0.09375
- fc2_bias: bfloat16 [2048], P('dp'), may hold values from -6 to 6
- cotangent: bfloat16 [8192, 2048], P(('dp', 'tensor')), may hold values from -6 to 6
Outputs:
- hidden_out: bfloat16 [8192, 2048], P(('dp', 'tensor'))
- input_grad: float32 [8192, 2048], P(('dp', 'tensor'))
- qkv_weight_grad: float32 [2048, 3, 2048], P('dp', None, 'tensor')
- qkv_bias_grad: float32 [3, 32, 64], P(None, 'tensor', 'dp')
- dense_weight_grad: float32 [2048, 2048], P('tensor', 'dp')
- dense_bias_grad: float32 [2048], P(('dp', 'tensor'))
- fc1_weight_grad: float32 [2048, 8192], P('dp', 'tensor')
- fc1_bias_grad: float32 [128, 64], P('tensor', 'dp')
- fc2_weight_grad: float32 [8192, 2048], P('tensor', 'dp')
- fc2_bias_grad: float32 [2048], P(('dp', 'tensor'))
- ln_gain_grad: float32 [2048], P(('dp', 'tensor'))
- ln_bias_grad: float32 [2048], P(('dp', 'tensor'))
All inputs are finite; a program needn't handle non-finite values.
Results may differ from a plain program's by a relative error of at most 0.013.
Values may be sent and summed in bfloat16 or wider, within the bound.
A program may use at most 256 MiB of HBM per device.

v0:
```python
import math

import jax
import jax.numpy as jnp
from jax import lax
from jax.sharding import PartitionSpec as P

HD = 64
ROT = 32
LEN = 512


EPSILON = 1e-05
GELU_C = math.sqrt(2.0 / math.pi)


def gelu_pair(hidden_pre):
    tanh_arg = GELU_C * (hidden_pre + 0.044715 * hidden_pre * hidden_pre * hidden_pre)
    tangent = jnp.tanh(tanh_arg)
    gelu_value = 0.5 * hidden_pre * (1.0 + tangent)
    gelu_slope = 0.5 * (1.0 + tangent) + 0.5 * hidden_pre * (1.0 - tangent * tangent) * GELU_C * (
        1.0 + 3.0 * 0.044715 * hidden_pre * hidden_pre
    )
    return (gelu_value, gelu_slope)


def rotary_tables(row_count):
    position = (jnp.arange(row_count) % LEN).astype(jnp.float32)
    frequency = 10000.0 ** (-jnp.arange(0, ROT, 2).astype(jnp.float32) / ROT)
    angles = position[:, None] * frequency[None, :]
    return (jnp.cos(angles)[:, None, :], jnp.sin(angles)[:, None, :])


def rotate(field_in, cosine, sine_table, sign_flip):
    half_rot = ROT // 2
    lower_half = field_in[..., :half_rot]
    upper_half = field_in[..., half_rot:ROT]
    return jnp.concatenate(
        [
            lower_half * cosine - sign_flip * upper_half * sine_table,
            upper_half * cosine + sign_flip * lower_half * sine_table,
            field_in[..., ROT:],
        ],
        axis=-1,
    )


def causal_scores(q_rot, k_rot):
    score_scale = 1.0 / math.sqrt(HD)
    scores = (
        jnp.einsum("qhd,khd->hqk", q_rot, k_rot, preferred_element_type=jnp.float32) * score_scale
    )
    causal = jnp.arange(LEN)[:, None] >= jnp.arange(LEN)[None, :]
    return jnp.where(causal, scores, -jnp.inf)


def attend_forward(inputs):
    q_rot, k_rot, v_rows = inputs
    scores = causal_scores(q_rot, k_rot)
    row_peak = jnp.max(scores, axis=-1, keepdims=True)
    log_total = row_peak + jnp.log(jnp.sum(jnp.exp(scores - row_peak), axis=-1, keepdims=True))
    probs_half = jnp.exp(scores - log_total).astype(jnp.bfloat16)
    context = jnp.einsum(
        "hqk,khd->qhd", probs_half, v_rows, preferred_element_type=jnp.float32
    ).astype(jnp.bfloat16)
    return (context, log_total)


def attend_backward(inputs):
    q_rot, k_rot, v_rows, context_grad, log_total = inputs
    score_scale = 1.0 / math.sqrt(HD)
    probs_full = jnp.exp(causal_scores(q_rot, k_rot) - log_total)
    probs_half = probs_full.astype(jnp.bfloat16)
    prob_grad = jnp.einsum("qhd,khd->hqk", context_grad, v_rows, preferred_element_type=jnp.float32)
    row_delta = jnp.sum(probs_full * prob_grad, axis=-1, keepdims=True)
    score_grad = (probs_full * (prob_grad - row_delta) * score_scale).astype(jnp.bfloat16)
    query_grad = jnp.einsum("hqk,khd->qhd", score_grad, k_rot, preferred_element_type=jnp.float32)
    key_grad = jnp.einsum("hqk,qhd->khd", score_grad, q_rot, preferred_element_type=jnp.float32)
    value_grad = jnp.einsum(
        "hqk,qhd->khd", probs_half, context_grad, preferred_element_type=jnp.float32
    )
    return (query_grad, key_grad, value_grad)


def shards(
    hidden_in,
    ln_gain,
    ln_bias,
    qkv_weight,
    qkv_bias,
    dense_weight,
    dense_bias,
    fc1_weight,
    fc1_bias,
    fc2_weight,
    fc2_bias,
    cotangent,
):
    gathered = (
        lax.all_gather(ln_gain, "dp", axis=0, tiled=True),
        lax.all_gather(ln_bias, "dp", axis=0, tiled=True),
        lax.all_gather(qkv_weight, "dp", axis=0, tiled=True),
        lax.all_gather(qkv_bias, "dp", axis=2, tiled=True),
        lax.all_gather(dense_weight, "dp", axis=1, tiled=True),
        lax.all_gather(dense_bias, "dp", axis=0, tiled=True),
        lax.all_gather(fc1_weight, "dp", axis=0, tiled=True),
        lax.all_gather(fc1_bias, "dp", axis=1, tiled=True),
        lax.all_gather(fc2_weight, "dp", axis=1, tiled=True),
        lax.all_gather(fc2_bias, "dp", axis=0, tiled=True),
    )
    gain_full, shift_full, w_qkv, b_qkv, w_dense, b_dense, w_up, b_up, w_down, b_down = gathered
    gain = gain_full.astype(jnp.float32)
    width = hidden_in.shape[1]
    x_full = hidden_in.astype(jnp.float32)
    average = jnp.mean(x_full, axis=-1, keepdims=True)
    centred = x_full - average
    inv_std = lax.rsqrt(jnp.mean(centred * centred, axis=-1, keepdims=True) + EPSILON)
    x_hat = centred * inv_std
    normed = (x_hat * gain + shift_full.astype(jnp.float32)).astype(jnp.bfloat16)
    normed_all = lax.all_gather(normed, "tensor", axis=0, tiled=True)
    group_rows = normed_all.shape[0]
    head_cols = w_qkv.shape[2]
    heads_local = head_cols // HD
    seq_local = group_rows // LEN
    shape_four = (seq_local, LEN, heads_local, HD)
    cosine, sine_table = rotary_tables(group_rows)
    qkv = jnp.dot(
        normed_all, w_qkv.reshape(width, 3 * head_cols), preferred_element_type=jnp.float32
    )
    qkv = (qkv + b_qkv.astype(jnp.float32).reshape(3 * head_cols)).reshape(
        group_rows, 3, heads_local, HD
    )
    q_rot = rotate(qkv[:, 0], cosine, sine_table, 1.0).astype(jnp.bfloat16).reshape(shape_four)
    k_rot = rotate(qkv[:, 1], cosine, sine_table, 1.0).astype(jnp.bfloat16).reshape(shape_four)
    v_rows = qkv[:, 2].astype(jnp.bfloat16).reshape(shape_four)
    context_seq, log_total = lax.map(attend_forward, (q_rot, k_rot, v_rows))
    context = context_seq.reshape(group_rows, head_cols)
    hidden_pre = jnp.dot(normed_all, w_up, preferred_element_type=jnp.float32) + b_up.astype(
        jnp.float32
    ).reshape(-1)
    gelu_value, gelu_slope = gelu_pair(hidden_pre)
    act_rows = gelu_value.astype(jnp.bfloat16)
    partial_value = jnp.dot(context, w_dense, preferred_element_type=jnp.float32) + jnp.dot(
        act_rows, w_down, preferred_element_type=jnp.float32
    )
    summed = lax.psum_scatter(
        partial_value.astype(jnp.bfloat16), "tensor", scatter_dimension=0, tiled=True
    ).astype(jnp.float32)
    hidden_out = (
        x_full + summed + b_dense.astype(jnp.float32) + b_down.astype(jnp.float32)
    ).astype(jnp.bfloat16)
    grad_all = lax.all_gather(cotangent, "tensor", axis=0, tiled=True)
    fc2_term = jnp.einsum("rf,rd->fd", act_rows, grad_all, preferred_element_type=jnp.float32)
    dense_term = jnp.einsum("rc,rd->cd", context, grad_all, preferred_element_type=jnp.float32)
    act_grad = jnp.einsum("rd,fd->rf", grad_all, w_down, preferred_element_type=jnp.float32)
    hidden_grad = act_grad * gelu_slope
    hidden_grad_b = hidden_grad.astype(jnp.bfloat16)
    fc1_bias_term = jnp.sum(hidden_grad, axis=0).reshape(-1, HD)
    fc1_term = jnp.einsum(
        "rd,rf->df", normed_all, hidden_grad_b, preferred_element_type=jnp.float32
    )
    context_grad = (
        jnp.einsum("rd,cd->rc", grad_all, w_dense, preferred_element_type=jnp.float32)
        .astype(jnp.bfloat16)
        .reshape(shape_four)
    )
    query_grad, key_grad, value_grad = lax.map(
        attend_backward, (q_rot, k_rot, v_rows, context_grad, log_total)
    )
    query_grad = rotate(query_grad.reshape(group_rows, heads_local, HD), cosine, sine_table, -1.0)
    key_grad = rotate(key_grad.reshape(group_rows, heads_local, HD), cosine, sine_table, -1.0)
    qkv_grad = jnp.stack(
        [query_grad, key_grad, value_grad.reshape(group_rows, heads_local, HD)], axis=1
    )
    qkv_bias_term = jnp.sum(qkv_grad, axis=0)
    qkv_grad_b = qkv_grad.astype(jnp.bfloat16).reshape(group_rows, 3 * head_cols)
    qkv_term = jnp.einsum(
        "rd,rc->dc", normed_all, qkv_grad_b, preferred_element_type=jnp.float32
    ).reshape(width, 3, head_cols)
    normed_grad = jnp.einsum("rf,df->rd", hidden_grad_b, w_up, preferred_element_type=jnp.float32)
    normed_grad = normed_grad + jnp.einsum(
        "rc,dc->rd",
        qkv_grad_b,
        w_qkv.reshape(width, 3 * head_cols),
        preferred_element_type=jnp.float32,
    )
    qkv_sum, qkv_bias_sum, dense_sum, fc1_sum, fc1_bias_sum, fc2_sum = (
        lax.psum_scatter(
            qkv_term.astype(jnp.bfloat16), "dp", scatter_dimension=0, tiled=True
        ).astype(jnp.float32),
        lax.psum_scatter(
            qkv_bias_term.astype(jnp.bfloat16), "dp", scatter_dimension=2, tiled=True
        ).astype(jnp.float32),
        lax.psum_scatter(
            dense_term.astype(jnp.bfloat16), "dp", scatter_dimension=1, tiled=True
        ).astype(jnp.float32),
        lax.psum_scatter(
            fc1_term.astype(jnp.bfloat16), "dp", scatter_dimension=0, tiled=True
        ).astype(jnp.float32),
        lax.psum_scatter(
            fc1_bias_term.astype(jnp.bfloat16), "dp", scatter_dimension=1, tiled=True
        ).astype(jnp.float32),
        lax.psum_scatter(
            fc2_term.astype(jnp.bfloat16), "dp", scatter_dimension=1, tiled=True
        ).astype(jnp.float32),
    )
    normed_local = lax.psum_scatter(normed_grad, "tensor", scatter_dimension=0, tiled=True)
    grad_local = cotangent.astype(jnp.float32)
    grad_hat = normed_local * gain
    input_grad = grad_local + inv_std * (
        grad_hat
        - jnp.mean(grad_hat, axis=-1, keepdims=True)
        - x_hat * jnp.mean(grad_hat * x_hat, axis=-1, keepdims=True)
    )
    small_sums = (
        lax.psum_scatter(
            jnp.sum(normed_local * x_hat, axis=0), ("dp", "tensor"), scatter_dimension=0, tiled=True
        ),
        lax.psum_scatter(
            jnp.sum(normed_local, axis=0), ("dp", "tensor"), scatter_dimension=0, tiled=True
        ),
        lax.psum_scatter(
            jnp.sum(grad_local, axis=0), ("dp", "tensor"), scatter_dimension=0, tiled=True
        ),
    )
    return (
        hidden_out,
        input_grad,
        qkv_sum,
        qkv_bias_sum,
        dense_sum,
        small_sums[2],
        fc1_sum,
        fc1_bias_sum,
        fc2_sum,
        small_sums[2],
        small_sums[0],
        small_sums[1],
    )


def solution(mesh):
    placed = (
        P(("dp", "tensor"), None),
        P("dp"),
        P("dp"),
        P("dp", None, "tensor"),
        P(None, "tensor", "dp"),
        P("tensor", "dp"),
        P("dp"),
        P("dp", "tensor"),
        P("tensor", "dp"),
        P("tensor", "dp"),
        P("dp"),
        P(("dp", "tensor"), None),
    )
    return jax.shard_map(
        shards,
        mesh=mesh,
        in_specs=placed,
        out_specs=(
            P(("dp", "tensor"), None),
            P(("dp", "tensor"), None),
            P("dp", None, "tensor"),
            P(None, "tensor", "dp"),
            P("tensor", "dp"),
            P(("dp", "tensor")),
            P("dp", "tensor"),
            P("tensor", "dp"),
            P("tensor", "dp"),
            P(("dp", "tensor")),
            P(("dp", "tensor")),
            P(("dp", "tensor")),
        ),
        check_vma=False,
    )
```

profile of v0, /device:TPU:0, one launch (start us, length us, event | category | flops | bytes accessed | tf_op | source)
XLA Modules:
  0.0 1050.0 jit_solution(10837101026190310447)
XLA Ops:
  47.8 75.3 %all-gather.21.cloned.1.call-done = bf16[1024,2048]{1,0:T(8,128)(2,1)} async-done(((bf16[256,2048]{1,0:T(8,128)(2,1)}), bf16[1024,2048]{1,0:T(8,128)(2,1)}) %all-gather.21.cloned.1.call-update) | async-done | bytes 4194320 | tf_op jit(solution)/shard_map/all_gather | solution.py:152
  132.0 72.5 %all-gather.11.cloned.1.call-done = bf16[1024,2048]{1,0:T(8,128)(2,1)} async-done(((bf16[256,2048]{1,0:T(8,128)(2,1)}), bf16[1024,2048]{1,0:T(8,128)(2,1)}) %all-gather.11.cloned.1.call-update) | async-done | bytes 4194320 | tf_op jit(solution)/shard_map/all_gather | solution.py:120
  204.5 46.8 %all-gather.13.cloned.1.call-done = bf16[2048,3,512]{0,2,1:T(8,128)(2,1)} async-done(((bf16[256,3,512]{0,2,1:T(8,128)(2,1)}), bf16[2048,3,512]{0,2,1:T(8,128)(2,1)}) %all-gather.13.cloned.1.call-update) | async-done | bytes 6291472 | tf_op jit(solution)/shard_map/all_gather | solution.py:102
  288.6 18.0 %while.26 = (s32[]{:T(128)}, bf16[2,512,8,64]{1,3,2,0:T(8,128)(2,1)}, f32[2,8,512,1]{2,1,3,0:T(8,128)S(1)}, bf16[2,512,8,64]{1,3,2,0:T(8,128)(2,1)}, bf16[2,512,...) while((s32[]{:T(128)}, bf16[2,512,8,64]{1,3,2,0:T(8,128)(2,1)}, ...), condition=%wide.region_5.6_spmd, body=%wide.region_2.5_spmd.sunk | while | flops 560459776 | bytes 36833424 | solution.py:136
  316.1 212.5 %while.27 = (s32[]{:T(128)}, f32[2,512,8,64]{1,0,3,2:T(2,128)}, f32[2,512,8,64]{1,0,3,2:T(2,128)}, f32[2,512,8,64]{1,0,3,2:T(2,128)}, bf16[2,512,8,64]{1,3,2,0:T...) while((s32[]{:T(128)}, f32[2,512,8,64]{1,0,3,2:T(2,128)}, ...), condition=%wide.region_9.10_spmd, body=%wide.region_7.9_spmd.sunk | while | flops 1396974592 | bytes 146917552 | solution.py:167
  326.4 19.7 %dynamic_update_slice.29 = f32[2,512,8,64]{1,0,3,2:T(2,128)} dynamic-update-slice(f32[2,512,8,64]{1,0,3,2:T(2,128)} %get-tuple-element.447, f32[1,512,8,64]{1,0,3,2:T(1,128)S(1)} %copy.176, s32[]{:T(128)S(6)} %copy.195, s32[]{:T(128)} %constant.74.clone.1..sunk, s32[]{:T(128)} %constant.74.clone.1..sunk, s32[]{:T(128)} %constant.74.clone.1..sunk) | dynamic-update-slice | bytes 2097156 | tf_op jit(solution)/shard_map/while/body/jit(dynamic_update_index_in_dim)/dynamic_update_slice | solution.py:167
  351.9 14.5 %fusion.179 = f32[1,512,8,64]{1,3,2,0:T(8,128)} fusion(f32[8,512,512]{1,2,0:T(8,128)} %fusion.176, f32[8,512,512]{1,2,0:T(8,128)} %copy-done, f32[8,512]{1,0:T(8,128)S(1)} %dynamic-slice_bitcast_fusion.2, pred[512,512]{0,1:T(8,128)(4,1)S(1)} %iota_compare_fusion.5, bf16[2,512,8,64]{1,3,2,0:T(8,128)(2,1)} %get-tuple-element.460, s32[]{:T(128)S(6)} %copy.195), kind=kOutput, calls=%fused_computation.43.clone.1 | convolution fusion | flops 291508736 | bytes 35684356 | tf_op jit(solution)/shard_map/while/body/eval_jaxpr/hqk,qhd->khd/dot_general | solution.py:78
  366.4 13.8 %fusion.178 = f32[1,512,8,64]{1,3,2,0:T(8,128)S(1)} fusion(f32[8,512,512]{1,2,0:T(8,128)} %fusion.176, f32[8,512,512]{1,2,0:T(8,128)} %copy-done, f32[8,512]{1,0:T(8,128)S(1)} %dynamic-slice_bitcast_fusion.2, pred[512,512]{0,1:T(8,128)(4,1)S(1)} %iota_compare_fusion.5, bf16[2,512,8,64]{1,3,2,0:T(8,128)(2,1)S(1)} %get-tuple-element.459, s32[]{:T(128)S(6)} %copy.195), kind=kOutput, calls=%fused_computation.42.clone.1 | convolution fusion | flops 291508736 | bytes 35684356 | tf_op jit(solution)/shard_map/while/body/eval_jaxpr/hqk,khd->qhd/dot_general | solution.py:77
  383.5 19.6 %dynamic_update_slice.28 = f32[2,512,8,64]{1,0,3,2:T(2,128)} dynamic-update-slice(f32[2,512,8,64]{1,0,3,2:T(2,128)} %get-tuple-element.446, f32[1,512,8,64]{1,0,3,2:T(1,128)S(1)} %copy.175, s32[]{:T(128)S(6)} %copy.195, s32[]{:T(128)} %constant.74.clone.1..sunk, s32[]{:T(128)} %constant.74.clone.1..sunk, s32[]{:T(128)} %constant.74.clone.1..sunk) | dynamic-update-slice | bytes 2097156 | tf_op jit(solution)/shard_map/while/body/jit(dynamic_update_index_in_dim)/dynamic_update_slice | solution.py:167
  403.2 19.6 %dynamic_update_slice.27 = f32[2,512,8,64]{1,0,3,2:T(2,128)} dynamic-update-slice(f32[2,512,8,64]{1,0,3,2:T(2,128)} %get-tuple-element.445, f32[1,512,8,64]{1,0,3,2:T(1,128)S(1)} %copy.174, s32[]{:T(128)S(6)} %copy.195, s32[]{:T(128)} %constant.74.clone.1..sunk, s32[]{:T(128)} %constant.74.clone.1..sunk, s32[]{:T(128)} %constant.74.clone.1..sunk) | dynamic-update-slice | bytes 2097156 | tf_op jit(solution)/shard_map/while/body/jit(dynamic_update_index_in_dim)/dynamic_update_slice | solution.py:167
  432.8 19.6 %dynamic_update_slice.29 = f32[2,512,8,64]{1,0,3,2:T(2,128)} dynamic-update-slice(f32[2,512,8,64]{1,0,3,2:T(2,128)} %get-tuple-element.447, f32[1,512,8,64]{1,0,3,2:T(1,128)S(1)} %copy.176, s32[]{:T(128)S(6)} %copy.195, s32[]{:T(128)} %constant.74.clone.1..sunk, s32[]{:T(128)} %constant.74.clone.1..sunk, s32[]{:T(128)} %constant.74.clone.1..sunk) | dynamic-update-slice | bytes 2097156 | tf_op jit(solution)/shard_map/while/body/jit(dynamic_update_index_in_dim)/dynamic_update_slice | solution.py:167
  458.2 14.5 %fusion.179 = f32[1,512,8,64]{1,3,2,0:T(8,128)} fusion(f32[8,512,512]{1,2,0:T(8,128)} %fusion.176, f32[8,512,512]{1,2,0:T(8,128)} %copy-done, f32[8,512]{1,0:T(8,128)S(1)} %dynamic-slice_bitcast_fusion.2, pred[512,512]{0,1:T(8,128)(4,1)S(1)} %iota_compare_fusion.5, bf16[2,512,8,64]{1,3,2,0:T(8,128)(2,1)} %get-tuple-element.460, s32[]{:T(128)S(6)} %copy.195), kind=kOutput, calls=%fused_computation.43.clone.1 | convolution fusion | flops 291508736 | bytes 35684356 | tf_op jit(solution)/shard_map/while/body/eval_jaxpr/hqk,qhd->khd/dot_general | solution.py:78
  489.3 19.6 %dynamic_update_slice.28 = f32[2,512,8,64]{1,0,3,2:T(2,128)} dynamic-update-slice(f32[2,512,8,64]{1,0,3,2:T(2,128)} %get-tuple-element.446, f32[1,512,8,64]{1,0,3,2:T(1,128)S(1)} %copy.175, s32[]{:T(128)S(6)} %copy.195, s32[]{:T(128)} %constant.74.clone.1..sunk, s32[]{:T(128)} %constant.74.clone.1..sunk, s32[]{:T(128)} %constant.74.clone.1..sunk) | dynamic-update-slice | bytes 2097156 | tf_op jit(solution)/shard_map/while/body/jit(dynamic_update_index_in_dim)/dynamic_update_slice | solution.py:167
  508.9 19.6 %dynamic_update_slice.27 = f32[2,512,8,64]{1,0,3,2:T(2,128)} dynamic-update-slice(f32[2,512,8,64]{1,0,3,2:T(2,128)} %get-tuple-element.445, f32[1,512,8,64]{1,0,3,2:T(1,128)S(1)} %copy.174, s32[]{:T(128)S(6)} %copy.195, s32[]{:T(128)} %constant.74.clone.1..sunk, s32[]{:T(128)} %constant.74.clone.1..sunk, s32[]{:T(128)} %constant.74.clone.1..sunk) | dynamic-update-slice | bytes 2097156 | tf_op jit(solution)/shard_map/while/body/jit(dynamic_update_index_in_dim)/dynamic_update_slice | solution.py:167
  566.5 16.2 %fusion.123 = f32[1024,2048]{1,0:T(8,128)} fusion(bf16[1024,2048]{1,0:T(8,128)(2,1)} %all-gather.11.cloned.1.call-done, bf16[2048,2048]{1,0:T(8,128)(2,1)} %all-gather.17.cloned.1.call-done), kind=kOutput, calls=%fused_computation.156 | convolution fusion | flops 8589934592 | bytes 20971520 | tf_op jit(solution)/shard_map/dot_general | solution.py:138
  582.7 18.3 %fusion.122 = (bf16[2048]{0:T(1024)(128)(2,1)S(1)}, bf16[1024,2048]{1,0:T(8,128)(2,1)S(1)}) fusion(f32[1024,2048]{1,0:T(8,128)} %fusion.123, f32[2048]{0:T(1024)S(1)} %reshape.199, bf16[1024,2048]{1,0:T(8,128)(2,1)} %all-gather.21.cloned.1.call-done, bf16[2048,2048]{1,0:T(8,128)(2,1)} %all-gather.19.cloned.1.call-done), kind=kOutput, calls=%fused_computation.155 | convolution fusion | flops 8633972736 | bytes 25178112 | tf_op jit(solution)/shard_map/rd,fd->rf/dot_general | solution.py:155
  614.7 16.1 %convolution_convert_fusion = bf16[2048,2048]{1,0:T(8,128)(2,1)} fusion(bf16[1024,2048]{1,0:T(8,128)(2,1)} %all-gather.21.cloned.1.call-done, f32[1024,2048]{1,0:T(8,128)} %fusion.123, f32[2048]{0:T(1024)S(1)} %reshape.199), kind=kOutput, calls=%fused_computation.85 | convolution fusion | flops 8615100416 | bytes 20979712 | tf_op jit(solution)/shard_map/rf,rd->fd/dot_general | solution.py:153
  630.8 14.8 %fusion.115 = f32[1024,2048]{1,0:T(8,128)S(1)} fusion(bf16[2048,2048]{1,0:T(8,128)(2,1)} %all-gather.17.cloned.1.call-done, bf16[1024,2048]{1,0:T(8,128)(2,1)} %copy-done.36), kind=kOutput, calls=%fused_computation.122 | convolution fusion | flops 8589934592 | bytes 20971520 | tf_op jit(solution)/shard_map/rf,df->rd/dot_general | solution.py:180
  656.7 16.2 %fusion.121 = f32[1024,2048]{1,0:T(8,128)S(1)} fusion(bf16[2048,2048]{1,0:T(8,128)(2,1)} %all-gather.19.cloned.1.call-done, f32[1024,2048]{1,0:T(8,128)} %fusion.123, f32[2048]{0:T(1024)S(1)} %reshape.199), kind=kOutput, calls=%fused_computation.154 | convolution fusion | flops 8610906112 | bytes 25174016 | tf_op jit(solution)/shard_map/dot_general | solution.py:143
  700.7 23.5 %all-reduce.6 = (bf16[3,8,64]{2,1,0:T(8,128)(2,1)S(1)}, bf16[32,64]{1,0:T(8,128)(2,1)S(1)}) all-reduce(bf16[3,8,64]{2,1,0:T(8,128)(2,1)S(1)} %fusion.95, bf16[32,64]{1,0:T(8,128)(2,1)S(1)} %convert_element_type.219), channel_id=5, replica_groups=mesh['dp'=8,'tensor'=4] {'dp'}, use_global_device_ids=true, to_apply=%region_15.16.clone | all-reduce | flops 3584 | bytes 14336
  731.0 37.7 %reduce-scatter.19.cloned.1.call-done = bf16[2048,256]{1,0:T(8,128)(2,1)} async-done(((bf16[2048,2048]{1,0:T(8,128)(2,1)}), bf16[2048,256]{1,0:T(8,128)(2,1)}) %reduce-scatter.19.cloned.1.call-update) | async-done | bytes 1048592 | tf_op jit(solution)/shard_map/reduce_scatter | solution.py:203
  771.3 144.3 %reduce-scatter.11.cloned.1.call-done = f32[256,2048]{1,0:T(8,128)} async-done(((f32[1024,2048]{1,0:T(8,128)}), f32[256,2048]{1,0:T(8,128)}) %reduce-scatter.11.cloned.1.call-update) | async-done | bytes 2097168 | tf_op jit(solution)/shard_map/reduce_scatter | solution.py:207
  918.2 77.0 %reduce-scatter.9.cloned.1.call-done = bf16[256,2048]{1,0:T(8,128)(2,1)} async-done(((bf16[1024,2048]{1,0:T(8,128)(2,1)}), bf16[256,2048]{1,0:T(8,128)(2,1)}) %reduce-scatter.9.cloned.1.call-update) | async-done | bytes 1048592 | tf_op jit(solution)/shard_map/reduce_scatter | solution.py:146
  1000.1 40.9 %all-reduce.5 = (f32[2048]{0:T(1024)S(1)}, f32[2048]{0:T(1024)S(1)}, f32[2048]{0:T(1024)S(1)}) all-reduce(f32[2048]{0:T(1024)S(1)} %get-tuple-element.296, f32[2048]{0:T(1024)S(1)} %get-tuple-element.243, f32[2048]{0:T(1024)S(1)} %get-tuple-element.246), channel_id=7, replica_groups=mesh['dp'=8,'tensor'=4] {'dp','tensor'}, use_global_device_ids=true, to_apply=%region_18.19.clone | all-reduce | flops 6144 | bytes 49152
  (227 shorter events, 273.2 us)
Async XLA Ops:
  7.2 28.7 %copy-start.16 = (bf16[256,3,512]{2,0,1:T(8,128)(2,1)S(1)}, bf16[256,3,512]{2,0,1:T(8,128)(2,1)}, u32[]{:S(2)}) copy-start(bf16[256,3,512]{2,0,1:T(8,128)(2,1)} %param.19) | copy-start | bytes 2359300
  7.2 31.2 %copy-start.27 = (bf16[3,8,8]{2,1,0:T(8,128)(2,1)S(1)}, bf16[3,8,8]{2,1,0:T(8,128)(2,1)}, u32[]{:S(2)}) copy-start(bf16[3,8,8]{2,1,0:T(8,128)(2,1)} %param.20) | copy-start | bytes 1156
  7.2 40.6 %all-gather.15.cloned.1.call-start = ((), (), s32[]{:S(2)}) async-start(), calls=%async_computation.8 | async-start | bytes 2359296 | tf_op jit(solution)/shard_map/all_gather | solution.py:104
  7.9 115.2 %all-gather.21.cloned.1.call-start = ((), (), s32[]{:S(2)}) async-start(), calls=%async_computation.12 | async-start | bytes 5242880 | tf_op jit(solution)/shard_map/all_gather | solution.py:152
  8.7 195.8 %all-gather.11.cloned.1.call-start = ((), (), s32[]{:S(2)}) async-start(), calls=%async_computation.6 | async-start | bytes 5242880 | tf_op jit(solution)/shard_map/all_gather | solution.py:120
  35.9 215.5 %all-gather.13.cloned.1.call-start = ((), (), s32[]{:S(2)}) async-start(), calls=%async_computation.7 | async-start | bytes 7077888 | tf_op jit(solution)/shard_map/all_gather | solution.py:102
  37.1 529.4 %all-gather.17.cloned.1.call-start = ((), (), s32[]{:S(2)}) async-start(), calls=%async_computation.9 | async-start | bytes 9437184 | tf_op jit(solution)/shard_map/all_gather | solution.py:106
  37.7 545.0 %all-gather.19.cloned.1.call-start = ((), (), s32[]{:S(2)}) async-start(), calls=%async_computation.10 | async-start | bytes 9437184 | tf_op jit(solution)/shard_map/all_gather | solution.py:108
  38.3 660.4 %reduce-scatter.15.cloned.1.call-start = ((), (), s32[]{:S(2)}) async-start(), calls=%async_computation.15 | async-start | bytes 2359296 | tf_op jit(solution)/shard_map/reduce_scatter | solution.py:194
  47.8 230.8 %copy-start.17 = (f32[1024,16]{0,1:T(8,128)}, f32[1024,16]{0,1:T(8,128)S(1)}, u32[]{:S(2)}) copy-start(f32[1024,16]{0,1:T(8,128)S(1)} %get-tuple-element.305) | copy-start | bytes 196612
  316.1 409.6 %reduce-scatter.13.cloned.1.call-start = ((), (), s32[]{:S(2)}) async-start(), calls=%async_computation.14 | async-start | bytes 7077888 | tf_op jit(solution)/shard_map/reduce_scatter | solution.py:188
  556.9 171.3 %reduce-scatter.17.cloned.1.call-start = ((), (), s32[]{:S(2)}) async-start(), calls=%async_computation.16 | async-start | bytes 9437184 | tf_op jit(solution)/shard_map/reduce_scatter | solution.py:197
  582.7 20.2 %copy-start.30 = (bf16[1024,2048]{1,0:T(8,128)(2,1)S(1)}, bf16[1024,2048]{1,0:T(8,128)(2,1)}, u32[]{:S(2)}) copy-start(bf16[1024,2048]{1,0:T(8,128)(2,1)} %all-gather.11.cloned.1.call-done) | copy-start | bytes 12582916
  614.6 154.0 %reduce-scatter.19.cloned.1.call-start = ((), (), s32[]{:S(2)}) async-start(), calls=%async_computation.17 | async-start | bytes 9437184 | tf_op jit(solution)/shard_map/reduce_scatter | solution.py:203
  630.8 284.8 %reduce-scatter.11.cloned.1.call-start = ((), (), s32[]{:S(2)}) async-start(), calls=%async_computation.13 | async-start | bytes 10485760 | tf_op jit(solution)/shard_map/reduce_scatter | solution.py:207
  656.6 16.3 %copy-start.13 = (bf16[64,8,2,512]{3,1,2,0:T(8,128)(2,1)S(1)}, bf16[64,8,2,512]{3,1,2,0:T(8,128)(2,1)}, u32[]{:S(2)}) copy-start(bf16[64,8,2,512]{3,1,2,0:T(8,128)(2,1)} %copy-done.12) | copy-start | bytes 3145732
  656.6 338.6 %reduce-scatter.9.cloned.1.call-start = ((), (), s32[]{:S(2)}) async-start(), calls=%async_computation.11 | async-start | bytes 5242880 | tf_op jit(solution)/shard_map/reduce_scatter | solution.py:146
  656.7 16.2 %copy-start.31 = (bf16[512,2048]{1,0:T(8,128)(2,1)S(1)}, bf16[512,2048]{1,0:T(8,128)(2,1)}, u32[]{:S(2)}) copy-start(bf16[512,2048]{1,0:T(8,128)(2,1)} %all-gather.15.cloned.1.call-done) | copy-start | bytes 6291460
  673.0 23.1 %copy-start.3 = (f32[1024,1,8,64]{0,3,2,1:T(8,128)S(1)}, f32[1024,1,8,64]{0,3,2,1:T(8,128)}, u32[]{:S(2)}) copy-start(f32[1024,1,8,64]{0,3,2,1:T(8,128)} %copy-done.2) | copy-start | bytes 6291460
  698.6 217.0 %copy-start.1 = (bf16[256,2048]{1,0:T(8,128)(2,1)S(1)}, bf16[256,2048]{1,0:T(8,128)(2,1)}, u32[]{:S(2)}) copy-start(bf16[256,2048]{1,0:T(8,128)(2,1)} %param.16) | copy-start | bytes 3145732
  698.6 217.0 %copy-start.22 = (f32[8,1,256]{2,1,0:T(1,128)S(1)}, f32[8,1,256]{2,1,0:T(1,128)}, u32[]{:S(2)}) copy-start(f32[8,1,256]{2,1,0:T(1,128)} %copy-done.21) | copy-start | bytes 24580
  698.7 217.0 %copy-start.24 = (f32[256]{0:T(256)S(1)}, f32[256]{0:T(256)}, u32[]{:S(2)}) copy-start(f32[256]{0:T(256)} %copy-done.23) | copy-start | bytes 3076
  698.7 217.0 %copy-start.26 = (f32[256]{0:T(256)S(1)}, f32[256]{0:T(256)}, u32[]{:S(2)}) copy-start(f32[256]{0:T(256)} %copy-done.25) | copy-start | bytes 3076
  698.7 296.5 %copy-start.9 = (bf16[256,2048]{1,0:T(8,128)(2,1)S(1)}, bf16[256,2048]{1,0:T(8,128)(2,1)}, u32[]{:S(2)}) copy-start(bf16[256,2048]{1,0:T(8,128)(2,1)} %param.27) | copy-start | bytes 3145732
  (30 other events, 120.3 us)
Sparse Core Ops, SparseCore 0:
  9.9 30.8 all-gather.14
  42.3 80.7 all-gather.20
  125.2 79.2 all-gather.10
  206.2 45.0 all-gather.12
  253.1 54.2 all-gather.16
  309.1 55.8 all-gather.18
  368.3 41.1 reduce-scatter.14
  557.0 61.9 reduce-scatter.12
  622.4 71.5 reduce-scatter.16
  697.3 71.2 reduce-scatter.18
  771.0 144.6 reduce-scatter.10
  917.8 77.3 reduce-scatter.8
where the time goes:
time: 1060 us; the launch traced here: 1050 us
  waiting for transfers between devices  456 us (43%)
  matrix products  231 us (22%)
  local copies, waits for them, and re-layouts  187 us (18%)
  blocking collectives  118 us (11%)
  other arithmetic  39.7 us (4%)
  between operations  15.8 us (1%)
    reduce_scatter x1, waiting for transfers between devices, shards(): lax.psum_scatter(normed_grad, 'tensor', scatter_dimension=0, tiled=True)  144 us
    dynamic_update_slice x12, local copies, waits for them, and re-layouts, shards(): lax.map(attend_backward, (q_rot, k_rot, v_rows, context_grad, log_total))  127 us
    reduce_scatter x1, waiting for transfers between devices, shards(): lax.psum_scatter(partial_value.astype(jnp.bfloat16), 'tensor', scatter_di...  77 us
    all_gather x1, waiting for transfers between devices, shards(): grad_all = lax.all_gather(cotangent, 'tensor', axis=0, tiled=True)  75.3 us
    all_gather x1, waiting for transfers between devices, shards(): normed_all = lax.all_gather(normed, 'tensor', axis=0, tiled=True)  72.5 us
    unnamed x2, blocking collectives  64.5 us
    all_gather x1, waiting for transfers between devices, shards(): lax.all_gather(qkv_weight, 'dp', axis=0, tiled=True)  46.8 us
    reduce_scatter x1, waiting for transfers between devices, shards(): lax.psum_scatter(fc2_term.astype(jnp.bfloat16), 'dp', scatter_dimension=1...  37.7 us
  transfers between devices with their start and end apart: 12, of which 6 were waited for; matrix products, arithmetic and copies ran while one was open for 41% of the time, Pallas kernels for 0%

commit v1 on v0

v1 whole, which is shorter than its diff:
```python
import functools
import math

import jax
import jax.numpy as jnp
import numpy as np
from jax import lax
from jax.experimental import pallas as pl
from jax.experimental.pallas import tpu as pltpu
from jax.sharding import PartitionSpec as P

HD = 64
ROT = 32
LEN = 512
EPSILON = 1e-05
GELU_C = math.sqrt(2.0 / math.pi)
F32 = jnp.float32
BF16 = jnp.bfloat16
ANY = pl.BlockSpec(memory_space=pl.ANY)
VMEM = pl.BlockSpec(memory_space=pltpu.VMEM)


def gelu_pair(h):
    square = h * h
    tangent = jnp.tanh(h * (GELU_C + (GELU_C * 0.044715) * square))
    half = 0.5 + 0.5 * tangent
    slope = half + 0.5 * h * (1.0 - tangent * tangent) * (GELU_C + (3.0 * 0.044715 * GELU_C) * square)
    return h * half, slope


def rotary_rows():
    position = np.arange(LEN, dtype=np.float32)
    frequency = (10000.0 ** (-np.arange(0, ROT, 2, dtype=np.float32) / ROT)).astype(np.float32)
    angles = (position[:, None] * frequency[None, :]).astype(np.float32)
    cosine, sine = np.cos(angles).astype(np.float32), np.sin(angles).astype(np.float32)
    rest = np.ones((LEN, HD - ROT), np.float32)
    none = np.zeros((LEN, ROT // 2), np.float32)
    here = np.concatenate([cosine, cosine, rest], axis=1)
    above = np.concatenate([-sine, none, 0 * rest], axis=1)
    below = np.concatenate([none, sine, 0 * rest], axis=1)
    return tuple(np.tile(part, (1, 2)) for part in (here, above, below))


def flip(index, mask):
    result, place = index, 1
    while place <= mask:
        if mask & place:
            result = result + (1 - 2 * ((index // place) % 2)) * place
        place *= 2
    return result


def span(bits):
    masks = [0]
    for bit in bits:
        masks = masks + [mask | (1 << bit) for mask in masks]
    return masks


def dot(a, b, dims):
    return lax.dot_general(a, b, (dims, ((), ())), preferred_element_type=F32)


NN, NT, TN = ((1,), (0,)), ((1,), (1,)), ((0,), (0,))


class Sizes:
    def __init__(self, groups, tensor, unit, width, hidden, heads_width):
        self.n, self.nt = groups, tensor
        self.bits = groups.bit_length() - 1
        self.unit, self.d, self.f, self.c = unit, width, hidden, heads_width
        self.rows = unit * tensor
        self.seqs = self.rows // LEN
        self.shard = width // groups
        self.q3 = 3 * heads_width
        self.n1 = self.q3 + hidden
        self.n2 = hidden + heads_width
        self.orders = (
            list(range(1, self.bits)) + [0],
            list(range(self.bits - 1, 0, -1)) + [0],
        )


def pack_rows(z):
    lanes = min(128, z.shard)
    per = z.shard // lanes
    return lanes, per, 4 * per, z.f // 128, z.q3 // 128


def rotated(tile, here, above, below):
    width = tile.shape[1]
    up = pltpu.roll(tile, width - ROT // 2, axis=1)
    down = pltpu.roll(tile, ROT // 2, axis=1)
    repeat = width // 128
    return (
        tile * jnp.tile(here, (1, repeat))
        + up * jnp.tile(above, (1, repeat))
        + down * jnp.tile(below, (1, repeat))
    )


def forward_kernel(z, compute, *refs):
    (x_hbm, c_hbm, wq_hbm, wu_hbm, wd_hbm, pack_hbm, t_here, t_above, t_below,
     normed_o, xhat_o, cot_o, qkv_o, act_o, hg_o, ctx_o, dctx_o, branch_o, w1_o, small_o,
     w, xs, xh, cs, qkv, act, hg, ctx, dctx, nm, slots, vec, bias, small,
     loc_sem, out_sem, pk_send, pk_recv, w_send, w_recv, z_send, z_recv) = refs
    n, nt, R = z.n, z.nt, z.unit
    me, t = lax.axis_index("dp"), lax.axis_index("tensor")

    barrier = pltpu.get_barrier_semaphore()
    for m in range(1, n):
        pl.semaphore_signal(barrier, inc=1, device_id={"dp": flip(me, m)}, device_id_type=pl.DeviceIdType.MESH)
    for step in (1, nt - 1):
        pl.semaphore_signal(barrier, inc=1, device_id={"tensor": lax.rem(t + step, nt)}, device_id_type=pl.DeviceIdType.MESH)
    pl.semaphore_wait(barrier, n - 1 + 2)

    waits = []

    def remote(src, dst, send, recv, where):
        return pltpu.make_async_remote_copy(
            src_ref=src, dst_ref=dst, send_sem=send, recv_sem=recv, device_id=where, device_id_type=pl.DeviceIdType.MESH
        )

    def pack_copy(m, receive):
        slot = slots.at[flip(me, m)] if receive else slots.at[me]
        return remote(pack_hbm, slot, pk_send.at[m], pk_recv.at[m], {"dp": flip(me, m)})

    for m in range(1, n):
        copy = pack_copy(m, False)
        copy.start()
        waits.append((None, copy))
    own_pack = pltpu.make_async_copy(pack_hbm, slots.at[me], loc_sem.at[0])
    own_pack.start()

    def rows_of(u):
        return pl.ds(pl.multiple_of(u * R, R), R)

    def line(buf, which, j, up, receive):
        src = (t - (j - 1)) if up else (t + (j - 1))
        got = (t - j) if up else (t + j)
        unit = got if receive else src
        to = (t + 1) if up else (t - 1)
        ref = buf.at[rows_of(unit), :]
        s = (which * 2 + (0 if up else 1)) * nt + j
        return remote(ref, ref, z_send.at[s], z_recv.at[s], {"tensor": to})

    def sends(j, up):
        return ((t < nt - 1) & (t >= j - 1)) if up else ((t > 0) & (t <= nt - j))

    def gets(j, up):
        return (t >= j) if up else (t <= nt - 1 - j)

    def line_send(buf, which, j, up, extra=None):
        cond = sends(j, up) if extra is None else sends(j, up) & extra

        @pl.when(cond)
        def _():
            line(buf, which, j, up, False).start()

    def line_recv(buf, which, j, up):
        @pl.when(gets(j, up))
        def _():
            line(buf, which, j, up, True).wait_recv()

    def line_sent(buf, which):
        for j in range(1, nt):
            for up in (True, False):
                @pl.when(sends(j, up))
                def _():
                    line(buf, which, j, up, False).wait_send()

    own_x = pltpu.make_async_copy(x_hbm, xs.at[rows_of(t), :], loc_sem.at[1])
    own_x.start()
    own_c = pltpu.make_async_copy(c_hbm, cs.at[rows_of(t), :], loc_sem.at[2])
    own_c.start()

    chunks = [(wq_hbm, 0, z.q3), (wu_hbm, z.q3, z.f), (wd_hbm, z.n1, z.n2)]

    def slot_ref(d, col, width):
        return w.at[pl.ds(pl.multiple_of(d * z.shard, z.shard), z.shard), pl.ds(col, width)]

    def w_copy(c, h, stage, m, receive):
        src_hbm, col, width = chunks[c]
        half = width // 2
        col = col + h * half
        bit = z.orders[h][stage]
        to = flip(me, 1 << bit)
        d = flip(me, m | (1 << bit)) if receive else flip(me, m)
        dst = slot_ref(d, col, half)
        src = dst
        if m == 0 and not receive:
            src = src_hbm.at[:, pl.ds(h * half, half)]
        s = (c * 2 + h) * n + (m | (1 << bit))
        return remote(src, dst, w_send.at[s], w_recv.at[s], {"dp": to})

    def w_start(c, stage):
        for h in (0, 1):
            for m in span(z.orders[h][:stage]):
                copy = w_copy(c, h, stage, m, False)
                copy.start()
                waits.append((None, copy))

    def w_wait(c, stage):
        for h in (0, 1):
            for m in span(z.orders[h][:stage]):
                w_copy(c, h, stage, m, True).wait_recv()

    for c, (src, col, width) in enumerate(chunks):
        pltpu.make_async_copy(src, slot_ref(me, col, width), loc_sem.at[3 + c]).start()

    w_start(0, 0)
    own_x.wait()
    line_send(xs, 0, 1, True)
    line_send(xs, 0, 1, False)
    w_start(1, 0)
    own_c.wait()

    def cot_starts(j):
        line_send(cs, 1, 1, True, t == j)
        line_send(cs, 1, 1, False, t == nt - 1 - j)

    cot_starts(0)

    def x_event(j):
        for up in (True, False):
            line_recv(xs, 0, j, up)
        if j < nt - 1:
            for up in (True, False):
                line_send(xs, 0, j + 1, up)
        cot_starts(j)

    def c_event(j):
        for up in (True, False):
            line_recv(cs, 1, j, up)
        if j < nt - 1:
            for up in (True, False):
                line_send(cs, 1, j + 1, up)

    for m in range(1, n):
        pack_copy(m, True).wait_recv()
    own_pack.wait()
    for c, (src, col, width) in enumerate(chunks):
        pltpu.make_async_copy(src, slot_ref(me, col, width), loc_sem.at[3 + c]).wait()

    outs = []

    def put(src, dst):
        copy = pltpu.make_async_copy(src, dst, out_sem.at[len(outs)])
        copy.start()
        outs.append(copy)

    last = z.bits - 1

    lanes, per, base, frows, qrows = pack_rows(z)

    def vectors():
        for v in range(4):
            for d in range(n):
                for r in range(per):
                    at = d * z.shard + r * lanes
                    vec[pl.ds(v, 1), pl.ds(at, lanes)] = slots[d, pl.ds(v * per + r, 1), :lanes].astype(F32)
        total = jnp.zeros((frows + qrows, 128), F32)
        for d in range(n):
            total = total + slots[d, pl.ds(base, frows + qrows), :].astype(F32)
        for r in range(qrows):
            bias[:, pl.ds(r * 128, 128)] = total[frows + r:frows + r + 1, :]
        for r in range(frows):
            bias[:, pl.ds(z.q3 + r * 128, 128)] = total[r:r + 1, :]

    def layer_norm(seq):
        block = 16

        def body(i, _):
            rows = pl.ds(pl.multiple_of(seq * LEN + i * block, block), block)
            full = xs[rows, :].astype(F32)
            centred = full - jnp.mean(full, axis=1, keepdims=True)
            inv_std = lax.rsqrt(jnp.mean(centred * centred, axis=1, keepdims=True) + EPSILON)
            hat = centred * inv_std
            xh[rows, :] = hat.astype(BF16)
            nm[rows, :] = (hat * vec[0:1, :] + vec[1:2, :]).astype(BF16)
            return 0

        lax.fori_loop(0, LEN // block, body, 0)

    def seq_rows(seq):
        return pl.ds(pl.multiple_of(seq * LEN, LEN), LEN)

    def qkv_tiles(seq):
        rows = seq_rows(seq)
        for part in range(3):
            cols = pl.ds(part * z.c, z.c)
            tile = dot(nm[rows, :], w[:, cols], NN) + bias[:, cols]
            if part < 2:
                tile = rotated(tile, t_here[...], t_above[...], t_below[...])
            qkv[rows, cols] = tile.astype(BF16)

    def up_tiles(seq, first, count):
        rows = seq_rows(seq)

        def body(j, _):
            cols = pl.ds(pl.multiple_of(j * 512, 512), 512)
            wcols = pl.ds(pl.multiple_of(z.q3 + j * 512, 512), 512)
            tile = dot(nm[rows, :], w[:, wcols], NN) + bias[:, wcols]
            value, slope = gelu_pair(tile)
            act[rows, cols] = value.astype(BF16)
            hg[rows, cols] = slope.astype(BF16)
            return 0

        lax.fori_loop(first, first + count, body, 0)

    half_rows = LEN // 2

    def attend(seq):
        low = lax.broadcasted_iota(jnp.int32, (half_rows, 128), 1) < HD

        def pair(p, _):
            def block(part, start, count):
                cols = pl.ds(pl.multiple_of(part * z.c + p * 128, 128), 128)
                return qkv[pl.ds(pl.multiple_of(seq * LEN + start, half_rows), count), cols]

            for qb in range(2):
                keys = half_rows * (qb + 1)
                q2 = block(0, qb * half_rows, half_rows) * BF16(0.125)
                k2 = block(1, 0, keys)
                v2 = block(2, 0, keys)
                row = lax.broadcasted_iota(jnp.int32, (half_rows, keys), 0) + qb * half_rows
                seen = lax.broadcasted_iota(jnp.int32, (half_rows, keys), 1) <= row
                parts = []
                for side in range(2):
                    q1 = jnp.where(low if side == 0 else ~low, q2, BF16(0))
                    scores = jnp.where(seen, dot(q1, k2, NT), -1e30)
                    peak = jnp.max(scores, axis=1, keepdims=True)
                    e = jnp.exp(scores - peak)
                    prob = e * (1.0 / jnp.sum(e, axis=1, keepdims=True))
                    parts.append(dot(prob.astype(BF16), v2, NN))
                out = jnp.where(low, parts[0], parts[1]).astype(BF16)
                ctx[pl.ds(pl.multiple_of(seq * LEN + qb * half_rows, half_rows), half_rows),
                    pl.ds(pl.multiple_of(p * 128, 128), 128)] = out
            return 0

        lax.fori_loop(0, z.c // 128, pair, 0)

    def branch_tiles(seq):
        rows = seq_rows(seq)

        def body(j, _):
            wrows = pl.ds(pl.multiple_of(j * 512, 512), 512)
            tile = dot(act[rows, :], w[wrows, pl.ds(z.n1, z.f)], NT)
            tile = tile + dot(ctx[rows, :], w[wrows, pl.ds(z.n1 + z.f, z.c)], NT)
            xs[rows, wrows] = tile.astype(BF16)
            return 0

        lax.fori_loop(0, z.d // 512, body, 0)

    def grad_tiles(seq):
        rows = seq_rows(seq)

        def body(j, _):
            cols = pl.ds(pl.multiple_of(j * 512, 512), 512)
            wcols = pl.ds(pl.multiple_of(z.n1 + j * 512, 512), 512)
            grad = dot(cs[rows, :], w[:, wcols], NN) * hg[rows, cols].astype(F32)
            small[1:2, cols] += jnp.sum(grad, axis=0, keepdims=True)
            hg[rows, cols] = grad.astype(BF16)
            return 0

        lax.fori_loop(0, z.f // 512, body, 0)
        dctx[rows, :] = dot(cs[rows, :], w[:, pl.ds(z.n1 + z.f, z.c)], NN).astype(BF16)

        def sums(i, _):
            part = cs[pl.ds(pl.multiple_of(seq * LEN + i * 64, 64), 64), :].astype(F32)
            small[0:1, :] += jnp.sum(part, axis=0, keepdims=True)
            return 0

        lax.fori_loop(0, LEN // 64, sums, 0)

    mine = t // (nt // z.seqs)
    other = z.seqs - 1 - mine
    if not compute:
        x_event(1)
        w_wait(0, 0); w_start(0, 1); w_start(2, 0)
        w_wait(1, 0); w_wait(0, 1); w_start(1, 1); w_start(0, 2)
        x_event(2)
        w_wait(2, 0); w_wait(1, 1); w_start(2, 1); w_start(1, 2)
        x_event(3)
        w_wait(0, 2); w_wait(1, 2); w_wait(2, 1); w_start(2, 2)
        c_event(1)
        w_wait(2, 2)
        c_event(2)
        c_event(3)
    else:
        small[...] = jnp.zeros_like(small)
        vectors()
        w_wait(0, 0); w_start(0, 1); w_start(2, 0)
        x_event(1)
        layer_norm(mine)
        w_wait(1, 0); w_wait(0, 1); w_start(1, 1); w_start(0, 2)
        w_wait(0, 2)
        qkv_tiles(mine)
        x_event(2)
        attend(mine)
        w_wait(2, 0); w_wait(1, 1); w_start(2, 1); w_start(1, 2)
        x_event(3)
        layer_norm(other)
        put(nm, normed_o); put(xh, xhat_o)
        qkv_tiles(other)
        put(qkv, qkv_o)
        w_wait(1, 2)
        put(w.at[:, pl.ds(0, z.n1)], w1_o)
        up_tiles(mine, 0, z.f // 512)
        c_event(1)
        w_wait(2, 1); w_start(2, 2)
        up_tiles(other, 0, z.f // 512)
        put(act, act_o)
        attend(other)
        put(ctx, ctx_o)
        w_wait(2, 2)
        line_sent(xs, 0)
        branch_tiles(mine)
        c_event(2)
        branch_tiles(other)
        put(xs, branch_o)
        grad_tiles(mine)
        c_event(3)
        put(cs, cot_o)
        grad_tiles(other)
        small[2:3, :z.d] = vec[0:1, :]
        small[3:4, :z.d] = vec[2:3, :] + vec[3:4, :]
        put(hg, hg_o); put(dctx, dctx_o); put(small, small_o)

    for cond, copy in waits:
        copy.wait_send()
    line_sent(cs, 1)
    if not compute:
        line_sent(xs, 0)
        put(xs, normed_o); put(xs, xhat_o); put(cs, cot_o); put(w.at[:, pl.ds(0, z.n1)], w1_o)
    for copy in outs:
        copy.wait()


def packed(z, ln_gain, ln_bias, dense_bias, fc2_bias, fc1_bias, qkv_bias):
    lanes, per, base, frows, qrows = pack_rows(z)
    me = lax.axis_index("dp")
    mine = jnp.arange(z.n)[None, :, None] == me
    def spread(a):
        rows, cols = a.reshape(-1, a.shape[-1]).shape
        return jnp.where(mine, a.reshape(rows, 1, cols), BF16(0)).reshape(-1, 128)
    plain = jnp.concatenate([v.reshape(per, lanes) for v in (ln_gain, ln_bias, dense_bias, fc2_bias)], axis=0)
    if lanes < 128:
        plain = jnp.pad(plain, ((0, 0), (0, 128 - lanes)))
    rows = jnp.concatenate([plain, spread(fc1_bias), spread(qkv_bias)], axis=0)
    return jnp.pad(rows, ((0, -rows.shape[0] % 16), (0, 0)))


def forward(z, compute, x, cot, wq, wu, wd, pack):
    prows = pack.shape[0]
    shape = lambda s, dt=BF16: jax.ShapeDtypeStruct(s, dt)
    T = z.rows
    outs = [shape((T, z.d)), shape((T, z.d)), shape((T, z.d)), shape((T, z.q3)), shape((T, z.f)), shape((T, z.f)),
            shape((T, z.c)), shape((T, z.c)), shape((T, z.d)), shape((z.d, z.n1)), shape((8, max(z.d, z.f)), F32)]
    v = pltpu.VMEM
    sem = pltpu.SemaphoreType.DMA
    scratch = [v((z.d, z.n1 + z.n2), BF16), v((T, z.d), BF16), v((T, z.d), BF16), v((T, z.d), BF16), v((T, z.q3), BF16),
               v((T, z.f), BF16), v((T, z.f), BF16), v((T, z.c), BF16), v((T, z.c), BF16), v((T, z.d), BF16),
               v((z.n, prows, 128), BF16), v((8, z.d), F32), v((1, z.n1), F32), v((8, max(z.d, z.f)), F32),
               sem((6,)), sem((12,)), sem((z.n,)), sem((z.n,)), sem((6 * z.n,)), sem((6 * z.n,)), sem((4 * z.nt,)), sem((4 * z.nt,))]
    return pl.pallas_call(
        functools.partial(forward_kernel, z, compute),
        out_shape=outs,
        in_specs=[ANY] * 6 + [VMEM] * 3,
        out_specs=[ANY] * len(outs),
        scratch_shapes=scratch,
        compiler_params=pltpu.CompilerParams(collective_id=0, has_side_effects=True, vmem_limit_bytes=67_043_328),
        name="forward_kernel",
    )(x, cot, wq, wu, wd, pack, *(jnp.asarray(p) for p in rotary_rows()))


def attention_backward(z, qkv, dctx):
    heads = z.c // HD
    four = (z.seqs, LEN, heads, HD)
    q, k, v = (qkv[:, i * z.c:(i + 1) * z.c].reshape(four) for i in range(3))
    g = dctx.reshape(four)
    seen = jnp.arange(LEN)[:, None] >= jnp.arange(LEN)[None, :]
    scores = jnp.einsum("sqhd,skhd->shqk", q, k, preferred_element_type=F32) * 0.125
    probs = jax.nn.softmax(jnp.where(seen, scores, -jnp.inf), axis=-1)
    grad = jnp.einsum("sqhd,skhd->shqk", g, v, preferred_element_type=F32)
    delta = jnp.sum(probs * grad, axis=-1, keepdims=True)
    ds = (probs * (grad - delta) * 0.125).astype(BF16)
    dq = jnp.einsum("shqk,skhd->sqhd", ds, k, preferred_element_type=F32)
    dk = jnp.einsum("shqk,sqhd->skhd", ds, q, preferred_element_type=F32)
    dv = jnp.einsum("shqk,sqhd->skhd", probs.astype(BF16), g, preferred_element_type=F32)
    here, above, below = (jnp.tile(jnp.asarray(p)[:, :HD], (z.seqs, 1)).reshape(z.seqs, LEN, 1, HD) for p in rotary_rows())
    def back(a):
        return a * here + jnp.roll(a * above, ROT // 2, axis=-1) + jnp.roll(a * below, -(ROT // 2), axis=-1)
    return jnp.concatenate([a.reshape(z.rows, z.c) for a in (back(dq), back(dk), dv)], axis=1)


def shards(x, ln_gain, ln_bias, qkv_weight, qkv_bias, dense_weight, dense_bias, fc1_weight, fc1_bias, fc2_weight, fc2_bias, cotangent):
    z = Sizes(lax.axis_size("dp"), lax.axis_size("tensor"), x.shape[0], x.shape[1], fc1_weight.shape[1], dense_weight.shape[0])
    pack = packed(z, ln_gain, ln_bias, dense_bias, fc2_bias, fc1_bias, qkv_bias)
    wd = jnp.concatenate([fc2_weight.T, dense_weight.T], axis=1)
    normed, xhat, cot, qkv, act, hg, ctx, dctx, branch, w1, small = forward(
        z, True, x, cotangent, qkv_weight.reshape(z.shard, z.q3), fc1_weight, wd, pack)
    scatter = lambda a, axis, dim: lax.psum_scatter(a, axis, scatter_dimension=dim, tiled=True)
    xf = x.astype(F32)
    centred = xf - jnp.mean(xf, axis=-1, keepdims=True)
    inv_std = lax.rsqrt(jnp.mean(centred * centred, axis=-1, keepdims=True) + EPSILON)
    hat = centred * inv_std
    gain = small[2:3, :z.d]
    hidden_out = (xf + scatter(branch, "tensor", 0).astype(F32) + small[3:4, :z.d]).astype(BF16)
    dqkv = attention_backward(z, qkv, dctx)
    dqkv_b = dqkv.astype(BF16)
    left = jnp.concatenate([dqkv_b, hg], axis=1)
    ngrad = jnp.dot(left, w1.T, preferred_element_type=F32)
    nl = scatter(ngrad.astype(BF16), "tensor", 0).astype(F32)
    gh = nl * gain
    input_grad = cotangent.astype(F32) + inv_std * (gh - jnp.mean(gh, -1, keepdims=True) - hat * jnp.mean(gh * hat, -1, keepdims=True))
    dw = lambda a, b: jnp.einsum("rd,rc->dc", a, b, preferred_element_type=F32).astype(BF16)
    d1 = scatter(dw(normed, left), "dp", 0).astype(F32)
    d2 = scatter(dw(cot, jnp.concatenate([act, ctx], axis=1)), "dp", 0).astype(F32)
    vecs = lax.psum(jnp.concatenate([small[0], small[1, :z.f], jnp.sum(dqkv, axis=0)]), "dp")
    lnv = lax.psum(jnp.stack([jnp.sum(nl * hat, axis=0), jnp.sum(nl, axis=0)]), ("dp", "tensor"))
    i, t = lax.axis_index("dp"), lax.axis_index("tensor")
    part = z.d // (z.n * z.nt)
    cut = lambda a: lax.dynamic_slice_in_dim(a, (i * z.nt + t) * part, part, 0)
    hc = HD // z.n
    dbias = cut(vecs[:z.d])
    fb = lax.dynamic_slice_in_dim(vecs[z.d:z.d + z.f].reshape(-1, HD), i * hc, hc, 1)
    qb = lax.dynamic_slice_in_dim(vecs[z.d + z.f:].reshape(3, -1, HD), i * hc, hc, 2)
    return (hidden_out, input_grad, d1[:, :z.q3].reshape(z.shard, 3, z.c), qb, d2[:, z.f:].T, dbias, d1[:, z.q3:], fb, d2[:, :z.f].T, dbias,
            cut(lnv[0]), cut(lnv[1]))


def solution(mesh):
    both = ("dp", "tensor")
    placed = (
        P(both, None), P("dp"), P("dp"), P("dp", None, "tensor"), P(None, "tensor", "dp"), P("tensor", "dp"),
        P("dp"), P("dp", "tensor"), P("tensor", "dp"), P("tensor", "dp"), P("dp"), P(both, None),
    )
    given = (
        P(both, None), P(both, None), P("dp", None, "tensor"), P(None, "tensor", "dp"), P("tensor", "dp"), P(both),
        P("dp", "tensor"), P("tensor", "dp"), P("tensor", "dp"), P(both), P(both), P(both),
    )
    return jax.shard_map(shards, mesh=mesh, in_specs=placed, out_specs=given, check_vma=False)
```

time: 1060 us -> 717 us (0.68)
  waiting for transfers between devices: 456 us -> 225 us
  Pallas kernels: 0 us -> 167 us
  local copies, waits for them, and re-layouts: 187 us -> 79.9 us
  matrix products: 231 us -> 135 us
  blocking collectives: 118 us -> 70 us
  other arithmetic: 39.7 us -> 15 us
    all_gather x6 -> x0, waiting for transfers between devices: 195 us -> none  [the longest x1 75.3 us: shards(): grad_all = lax.all_gather(cotangent, 'tensor', axis=0, tiled=True)]
    pallas_call x0 -> x1, Pallas kernels: none -> 167 us  [forward(): pl.pallas_call(functools.partial(forward_kernel, z, compute), out_shape=o...]
    dynamic_update_slice x12 -> x0, local copies, waits for them, and re-layouts: 127 us -> none  [shards(): lax.map(attend_backward, (q_rot, k_rot, v_rows, context_grad, log_total))]
    dot_general x26 -> x7, matrix products: 231 us -> 125 us  [the longest x2 38.3 us: shards(): jnp.einsum('rd,rc->dc', a, b, preferred_element_type=F32).astype(BF16)]
    psum x0 -> x2, blocking collectives: none -> 70 us  [the longest x1 46 us: shards(): lax.psum(jnp.stack([jnp.sum(nl * hat, axis=0), jnp.sum(nl, axis=0)]), ('d...]
    unnamed x2 -> x0, blocking collectives: 64.5 us -> none
    all_gather x6 -> x0, blocking collectives: 53.9 us -> none  [the longest x1 10.4 us: shards(): lax.all_gather(ln_bias, 'dp', axis=0, tiled=True)]
    reduce_scatter x6 -> x4, waiting for transfers between devices: 259 us -> 224 us  [shards(): lax.psum_scatter(a, axis, scatter_dimension=dim, tiled=True)]
  transfers between devices with their start and end apart: 12 -> 4, of which waited for: 6 -> 4; matrix products, arithmetic and copies ran while one was open for 41% -> 8% of each run, Pallas kernels for 0% -> 0%
where the time goes in v1:
time: 717 us; the launch traced here: 707 us
  waiting for transfers between devices  225 us (31%)
  Pallas kernels  167 us (23%)
  matrix products  135 us (19%)
  local copies, waits for them, and re-layouts  79.9 us (11%)
  blocking collectives  70 us (10%)
  other arithmetic  15 us (2%)
  between operations  14.6 us (2%)
    reduce_scatter x4, waiting for transfers between devices, shards(): lax.psum_scatter(a, axis, scatter_dimension=dim, tiled=True)  224 us
    pallas_call x1, Pallas kernels, forward(): pl.pallas_call(functools.partial(forward_kernel, z, compute), out_shape=o...  167 us
    psum x1, blocking collectives, shards(): lax.psum(jnp.stack([jnp.sum(nl * hat, axis=0), jnp.sum(nl, axis=0)]), ('d...  46 us
    dot_general x2, matrix products, shards(): jnp.einsum('rd,rc->dc', a, b, preferred_element_type=F32).astype(BF16)  38.3 us
    dot_general x1, matrix products, attention_backward(): dq = jnp.einsum('shqk,skhd->sqhd', ds, k, preferred_element_type=F32)  25.8 us
    psum x1, blocking collectives, shards(): lax.psum(jnp.concatenate([small[0], small[1, :z.f], jnp.sum(dqkv, axis=0)...  24 us
    dot_general x1, matrix products, attention_backward(): dk = jnp.einsum('shqk,sqhd->skhd', ds, q, preferred_element_type=F32)  23.6 us
    reshape x6, local copies, waits for them, and re-layouts, attention_backward(): a.reshape(z.rows, z.c)  23.4 us
  transfers between devices with their start and end apart: 4, of which 4 were waited for; matrix products, arithmetic and copies ran while one was open for 8% of the time, Pallas kernels for 0%

profile of v1, /device:TPU:0, one launch (start us, length us, event | category | flops | bytes accessed | tf_op | source)
XLA Modules:
  0.0 706.6 jit_solution(8624519381407287332)
XLA Ops:
  16.1 166.7 %forward_kernel.1 = (bf16[1024,2048]{1,0:T(8,128)(2,1)}, bf16[1024,2048]{1,0:T(8,128)(2,1)}, bf16[1024,2048]{1,0:T(8,128)(2,1)}, bf16[1024,1536]{1,0:T(8,128)(2,...) custom-call(bf16[256,2048]{1,0:T(8,128)(2,1)} %refs_0_.1, ...), custom_call_target="tpu_custom_call" | custom-call | tf_op jit(solution)/shard_map/forward_kernel/pallas_call | solution.py:466
  187.0 3.6 fusion.57
  198.4 3.9 reshape.151
  202.3 3.7 copy.63
  206.0 8.0 %fusion.38 = f32[2,8,512,512]{2,3,1,0:T(8,128)} fusion(bf16[2,512,8,64]{1,3,2,0:T(8,128)(2,1)S(1)} %copy.61, bf16[2,512,8,64]{3,2,1,0:T(8,128)(2,1)S(1)} %reshape.147), kind=kOutput, calls=%fused_computation.55 | convolution fusion | flops 536870912 | bytes 18874368 | tf_op jit(solution)/shard_map/sqhd,skhd->shqk/dot_general | solution.py:485
  214.1 10.7 %fusion.61 = (f32[2,8,512]{2,1,0:T(8,128)S(1)}, f32[2,8,512,512]{2,3,1,0:T(8,128)}) fusion(pred[512,512]{0,1:T(8,128)(4,1)S(1)} %copy-done.11, bf16[2,512,8,64]{1,3,2,0:T(8,128)(2,1)} %copy.57, bf16[2,512,8,64]{1,3,2,0:T(8,128)(2,1)} %copy.63), kind=kOutput, calls=%fused_computation.94 | convolution fusion | flops 553648640 | bytes 19169280 | tf_op jit(solution)/shard_map/sub | solution.py:484
  224.8 9.8 %fusion.42 = f32[2,512,8,64]{1,3,2,0:T(8,128)} fusion(bf16[2,512,8,64]{1,3,2,0:T(8,128)(2,1)S(1)} %copy.61, f32[2,8,512,512]{2,3,1,0:T(8,128)} %get-tuple-element.84, f32[2,8,512]{2,1,0:T(8,128)S(1)} %get-tuple-element.83), kind=kOutput, calls=%fused_computation.58 | convolution fusion | flops 545259520 | bytes 19955712 | tf_op jit(solution)/shard_map/shqk,sqhd->skhd/dot_general | solution.py:490
  234.7 23.6 %fusion.12 = f32[2,8,64,512]{3,2,1,0:T(8,128)} fusion(bf16[2,512,8,64]{1,3,2,0:T(8,128)(2,1)S(1)} %copy-done.9, f32[2,8,512,512]{2,3,1,0:T(8,128)} %fusion.38, f32[2,8,512,512]{2,3,1,0:T(8,128)} %get-tuple-element.84, f32[2,8,512]{2,1,0:T(8,128)S(1)} %get-tuple-element.83), kind=kOutput, calls=%fused_computation.17 | convolution fusion | flops 566239744 | bytes 36732928 | tf_op jit(solution)/shard_map/shqk,sqhd->skhd/dot_general | solution.py:489
  258.3 25.8 %bitcast_multiply_fusion.3 = (f32[2,512,8,64]{1,3,2,0:T(8,128)}, f32[2,512,8,64]{1,3,2,0:T(8,128)}, f32[2,512,8,64]{1,3,2,0:T(8,128)}, f32[2,512,8,64]{1,3,2,0:T(8,128)S(1)}, f32[2,8,64,512]{3,2,1,0:T(8,128)}) fusion(f32[512,64]{0,1:T(8,128)S(1)} %copy-done.19, f32[512,64]{0,1:T(8,128)S(1)} %copy-done.20, f32[2,8,64,512]{3,2,1,0:T(8,128)} %fusion.12, ...), kind=kOutput, calls=%fused_computation.52 | convolution fusion | flops 568336896 | bytes 47480832 | tf_op jit(solution)/shard_map/shqk,skhd->sqhd/dot_general | solution.py:488
  295.2 3.6 reshape.149
  298.8 3.8 copy.87
  302.6 4.8 reshape.150
  307.4 3.8 copy.85
  311.2 4.8 reshape.148
  321.6 19.0 %fusion.21 = bf16[1024,2048]{1,0:T(8,128)(2,1)} fusion(bf16[2048,3584]{1,0:T(8,128)(2,1)} %get-tuple-element.27, bf16[1024,2048]{1,0:T(8,128)(2,1)S(1)} %copy-done.18, bf16[1024,1536]{1,0:T(8,128)(2,1)S(1)} %get-tuple-element.61), kind=kOutput, calls=%fused_computation.23 | convolution fusion | flops 15049162752 | bytes 26214400 | tf_op jit(solution)/shard_map/dot_general | solution.py:513
  341.5 16.8 %convolution_convert_fusion.1 = bf16[2048,2560]{1,0:T(8,128)(2,1)} fusion(bf16[1024,2048]{1,0:T(8,128)(2,1)} %get-tuple-element.29, bf16[1024,512]{1,0:T(8,128)(2,1)} %get-tuple-element.31, bf16[1024,2048]{1,0:T(8,128)(2,1)} %get-tuple-element.30), kind=kOutput, calls=%fused_computation.9 | convolution fusion | flops 10753146880 | bytes 19922944 | tf_op jit(solution)/shard_map/rd,rc->dc/dot_general | solution.py:517
  358.4 21.5 %convolution_convert_fusion = bf16[2048,3584]{1,0:T(8,128)(2,1)} fusion(bf16[1024,2048]{1,0:T(8,128)(2,1)} %get-tuple-element.28, bf16[1024,2048]{1,0:T(8,128)(2,1)} %get-tuple-element.26, bf16[1024,1536]{1,0:T(8,128)(2,1)S(1)} %get-tuple-element.61), kind=kOutput, calls=%fused_computation.7 | convolution fusion | flops 15054405632 | bytes 26214400 | tf_op jit(solution)/shard_map/rd,rc->dc/dot_general | solution.py:517
  380.8 24.0 %psum.14 = f32[5632]{0:T(1024)S(1)} all-reduce(f32[5632]{0:T(1024)S(1)} %pad_maximum_fusion.6), channel_id=1, replica_groups=mesh['dp'=8,'tensor'=4] {'dp'}, use_global_device_ids=true, to_apply=%region_11.12 | all-reduce | flops 5632 | bytes 45056 | tf_op jit(solution)/shard_map/psum | solution.py:520
  407.1 9.7 %reduce-scatter.7.cloned.1.call-done = bf16[256,2048]{1,0:T(8,128)(2,1)} async-done(((bf16[1024,2048]{1,0:T(8,128)(2,1)}), bf16[256,2048]{1,0:T(8,128)(2,1)}) %reduce-scatter.7.cloned.1.call-update) | async-done | bytes 1048592 | tf_op jit(solution)/shard_map/reduce_scatter | solution.py:503
  419.1 46.0 %psum.15 = f32[2,2048]{1,0:T(2,128)S(1)} all-reduce(f32[2,2048]{1,0:T(2,128)S(1)} %pad_maximum_fusion.7), channel_id=1, replica_groups=mesh['dp'=8,'tensor'=4] {'dp','tensor'}, use_global_device_ids=true, to_apply=%region_15.16 | all-reduce | flops 4096 | bytes 32768 | tf_op jit(solution)/shard_map/psum | solution.py:521
  465.7 31.8 %reduce-scatter.5.cloned.1.call-done = bf16[256,2048]{1,0:T(8,128)(2,1)} async-done(((bf16[1024,2048]{1,0:T(8,128)(2,1)}), bf16[256,2048]{1,0:T(8,128)(2,1)}) %reduce-scatter.5.cloned.1.call-update) | async-done | bytes 1048592 | tf_op jit(solution)/shard_map/reduce_scatter | solution.py:503
  497.5 4.3 fusion.30
  501.8 81.6 %reduce-scatter.11.cloned.1.call-done = bf16[256,2560]{1,0:T(8,128)(2,1)} async-done(((bf16[2048,2560]{1,0:T(8,128)(2,1)}), bf16[256,2560]{1,0:T(8,128)(2,1)}) %reduce-scatter.11.cloned.1.call-update) | async-done | bytes 1310736 | tf_op jit(solution)/shard_map/reduce_scatter | solution.py:503
  590.5 100.9 %reduce-scatter.9.cloned.1.call-done = bf16[256,3584]{1,0:T(8,128)(2,1)} async-done(((bf16[2048,3584]{1,0:T(8,128)(2,1)}), bf16[256,3584]{1,0:T(8,128)(2,1)}) %reduce-scatter.9.cloned.1.call-update) | async-done | bytes 1835024 | tf_op jit(solution)/shard_map/reduce_scatter | solution.py:503
  (114 shorter events, 59.6 us)
Async XLA Ops:
  7.2 6.4 copy-start.10
  7.2 409.6 %reduce-scatter.7.cloned.1.call-start = ((), (), s32[]{:S(2)}) async-start(), calls=%async_computation.5 | async-start | bytes 5242880 | tf_op jit(solution)/shard_map/reduce_scatter | solution.py:503
  7.2 7.0 copy-start.14
  7.2 7.0 copy-start.15
  7.3 7.0 copy-start.16
  7.3 7.0 copy-start.17
  206.0 8.0 %copy-start.11 = (pred[512,512]{0,1:T(8,128)(4,1)S(1)}, pred[512,512]{0,1:T(8,128)(4,1)}, u32[]{:S(2)}) copy-start(pred[512,512]{0,1:T(8,128)(4,1)} %iota_compare_fusion) | copy-start | bytes 786436
  224.8 9.9 %copy-start.9 = (bf16[2,512,8,64]{1,3,2,0:T(8,128)(2,1)S(1)}, bf16[2,512,8,64]{1,3,2,0:T(8,128)(2,1)}, u32[]{:S(2)}) copy-start(bf16[2,512,8,64]{1,3,2,0:T(8,128)(2,1)} %copy.57) | copy-start | bytes 3145732
  234.7 23.6 %copy-start.8 = (bf16[2,512,8,64]{1,3,2,0:T(8,128)(2,1)S(1)}, bf16[2,512,8,64]{1,3,2,0:T(8,128)(2,1)}, u32[]{:S(2)}) copy-start(bf16[2,512,8,64]{1,3,2,0:T(8,128)(2,1)} %copy.63) | copy-start | bytes 3145732
  234.7 23.6 %copy-start.19 = (f32[512,64]{0,1:T(8,128)S(1)}, f32[512,64]{0,1:T(8,128)}, u32[]{:S(2)}) copy-start(f32[512,64]{0,1:T(8,128)} %constant.52) | copy-start | bytes 393220
  234.7 23.6 %copy-start.20 = (f32[512,64]{0,1:T(8,128)S(1)}, f32[512,64]{0,1:T(8,128)}, u32[]{:S(2)}) copy-start(f32[512,64]{0,1:T(8,128)} %constant.51) | copy-start | bytes 393220
  284.1 3.0 copy-start.5
  285.4 2.2 copy-start.4
  287.6 1.6 copy-start.6
  287.6 2.2 copy-start.7
  287.6 2.2 copy-start.12
  319.5 2.2 copy-start.18
  340.7 156.8 %reduce-scatter.5.cloned.1.call-start = ((), (), s32[]{:S(2)}) async-start(), calls=%async_computation.4 | async-start | bytes 5242880 | tf_op jit(solution)/shard_map/reduce_scatter | solution.py:503
  341.4 242.0 %reduce-scatter.11.cloned.1.call-start = ((), (), s32[]{:S(2)}) async-start(), calls=%async_computation.7 | async-start | bytes 11796480 | tf_op jit(solution)/shard_map/reduce_scatter | solution.py:503
  358.3 333.1 %reduce-scatter.9.cloned.1.call-start = ((), (), s32[]{:S(2)}) async-start(), calls=%async_computation.6 | async-start | bytes 16515072 | tf_op jit(solution)/shard_map/reduce_scatter | solution.py:503
  379.9 26.5 %copy-start = (bf16[256,2048]{1,0:T(8,128)(2,1)S(1)}, bf16[256,2048]{1,0:T(8,128)(2,1)}, u32[]{:S(2)}) copy-start(bf16[256,2048]{1,0:T(8,128)(2,1)} %refs_0_.1) | copy-start | bytes 3145732
  379.9 117.5 %copy-start.3 = (bf16[256,2048]{1,0:T(8,128)(2,1)S(1)}, bf16[256,2048]{1,0:T(8,128)(2,1)}, u32[]{:S(2)}) copy-start(bf16[256,2048]{1,0:T(8,128)(2,1)} %refs_1_.1) | copy-start | bytes 3145732
  404.8 294.2 %copy-start.21 = (f32[64]{0:T(128)}, f32[64]{0:T(128)S(1)}, u32[]{:S(2)}) copy-start(f32[64]{0:T(128)S(1)} %dynamic_slice.20) | copy-start | bytes 772
  693.9 3.6 copy-start.2
  (2 other events, 2.4 us)
Sparse Core Ops, SparseCore 0:
  340.8 75.9 reduce-scatter.6
  419.1 78.3 reduce-scatter.4
  501.0 82.4 reduce-scatter.10
  586.8 104.5 reduce-scatter.8
